TPU v7x, 32 devices: a whole 2x2x4 slice. The times are simulated.
32 devices in a mesh: seq: 16 (over z, x, core), head: 2 (over y).
Axes of the slice: x: 2, y: 2, z: 4, core: 2. Of those that a mesh axis runs over, the one named last changes fastest.
Arguments:
- query_rows: bfloat16 [3072, 2048], P('seq', 'head'), may hold values from -6 to 6
- key_rows: bfloat16 [3072, 2048], P('seq', 'head'), may hold values from -6 to 6
- value_rows: bfloat16 [3072, 2048], P('seq', 'head'), may hold values from -6 to 6
- grad_output: bfloat16 [3072, 2048], P('seq', 'head'), may hold values from -6 to 6
- positions: int32 [3072], P('seq'), may hold values from 0 to 3071, each once
Outputs:
- grad_query: bfloat16 [3072, 2048], P(('seq', 'head'))
- grad_keys: bfloat16 [3072, 2048], P('seq', 'head')
- grad_values: bfloat16 [3072, 2048], P('seq', 'head')
Inputs may be any that keep to these rules, and one draw needn't show every extreme that they name: `positions`: each number from 0 to 3071 appears once.
All inputs are finite; a program needn't handle non-finite values.
Results may differ from a plain program's by a relative error of at most 0.012.
Values may be sent and summed in bfloat16 or wider, within the bound.
A program may use at most 128 MiB of HBM per device.

v0:
```python
import functools

import jax
import jax.numpy as jnp
from jax import lax
from jax.experimental import pallas as pl
from jax.experimental.pallas import tpu as pltpu
from jax.sharding import PartitionSpec as P

HEAD_DIM = 128
MESH = pl.DeviceIdType.MESH
NT = (((1,), (1,)), ((), ()))
TN = (((0,), (0,)), ((), ()))


def kernel(
    members, heads, groups, rows, width,
    pos_ref, q_hbm, k_hbm, v_hbm, g_hbm,
    dq_out, dk_out, dv_out,
    qg_buf, kv_buf, qg_stage, kv_stage, pos_buf, key_pos, tops,
    z_buf, p_buf, dq_acc, part_stage, part_mates, kv_final, kv_back, dq_stage, dq_back,
    qg_local, kv_local, qg_send, qg_recv, kv_send, kv_recv, pos_send, pos_recv,
    mate_send, mate_recv, part_send, part_recv, back_send, back_recv, dq_send, dq_recv,
):
    ratio = members // heads
    me = lax.axis_index("seq")
    group = lax.axis_index("head")
    mine = me // ratio
    lane = lax.rem(me, ratio)
    scaling = HEAD_DIM ** (-0.5)
    block = heads * rows
    part_rows = rows // groups
    my_slot = lane * heads + mine

    def columns(index):
        return pl.ds(pl.multiple_of(index * HEAD_DIM, HEAD_DIM), HEAD_DIM)

    def local_copies(arrays, stage, first, sems, j):
        other = lax.rem(mine + j, heads)
        return [
            pltpu.make_async_copy(
                array.at[:, columns(other)],
                first.at[a] if j == 0 else stage.at[j, a],
                sems.at[a, j],
            )
            for a, array in enumerate(arrays)
        ]

    qg_locals = [
        local_copies((q_hbm, g_hbm), qg_stage, qg_buf.at[mine], qg_local, j) for j in range(heads)
    ]
    kv_locals = [
        local_copies((k_hbm, v_hbm), kv_stage, kv_buf.at[my_slot], kv_local, j)
        for j in range(heads)
    ]
    for copies in qg_locals[1:] + kv_locals[1:] + qg_locals[:1] + kv_locals[:1]:
        for copy in copies:
            copy.start()

    barrier = pltpu.get_barrier_semaphore()
    for d in range(1, members):
        pl.semaphore_signal(
            barrier, inc=1,
            device_id={"seq": lax.rem(me + d, members), "head": group}, device_id_type=MESH,
        )
    for e in range(1, groups):
        for j in range(heads):
            pl.semaphore_signal(
                barrier, inc=1,
                device_id={
                    "seq": lax.rem(mine + j, heads) * ratio + lane,
                    "head": lax.rem(group + e, groups),
                },
                device_id_type=MESH,
            )
    pl.semaphore_wait(barrier, members - 1 + (groups - 1) * heads)

    def qg_copy(j):
        return pltpu.make_async_remote_copy(
            src_ref=qg_stage.at[j], dst_ref=qg_buf.at[mine],
            send_sem=qg_send.at[j], recv_sem=qg_recv.at[j],
            device_id={"seq": lax.rem(mine + j, heads) * ratio + lane, "head": group},
            device_id_type=MESH,
        )

    def kv_copy(j):
        return pltpu.make_async_remote_copy(
            src_ref=kv_stage.at[j], dst_ref=kv_buf.at[my_slot],
            send_sem=kv_send.at[j], recv_sem=kv_recv.at[j],
            device_id={"seq": lax.rem(mine + j, heads) * ratio + lane, "head": group},
            device_id_type=MESH,
        )

    def pos_copy(d):
        return pltpu.make_async_remote_copy(
            src_ref=pos_ref, dst_ref=pos_buf.at[my_slot],
            send_sem=pos_send.at[d], recv_sem=pos_recv.at[d],
            device_id={"seq": lax.rem(me + d, members), "head": group}, device_id_type=MESH,
        )

    for d in range(1, members):
        pos_copy(d).start()
    for j in range(1, heads):
        for copy in qg_locals[j]:
            copy.wait()
        qg_copy(j).start()
    for j in range(1, heads):
        for copy in kv_locals[j]:
            copy.wait()
        kv_copy(j).start()

    def mate_copy(m, j):
        slot = lane * heads + lax.rem(mine + heads - j, heads)
        return pltpu.make_async_remote_copy(
            src_ref=kv_buf.at[slot], dst_ref=kv_buf.at[slot],
            send_sem=mate_send.at[m, j], recv_sem=mate_recv.at[m, j],
            device_id={"seq": mine * ratio + lax.rem(lane + m, ratio), "head": group},
            device_id_type=MESH,
        )

    pos_buf[my_slot] = pos_ref[...]
    for d in range(1, members):
        pos_copy(d).wait()

    def spread(slot, carry):
        row = jnp.broadcast_to(pos_buf[slot][0:1, :], (HEAD_DIM, width))
        key_pos[slot] = row.T[:rows]
        return carry

    lax.fori_loop(0, members, spread, 0)
    held = key_pos[pl.ds(lane * heads, heads)].reshape(block, HEAD_DIM)
    pos_row = held.T[0:1, :]
    for copy in qg_locals[0] + kv_locals[0]:
        copy.wait()
    for j in range(1, heads):
        qg_copy(j).wait()

    def eights(values):
        return values.reshape(rows // 8, 8, block)

    def stats(slot, carry):
        top, total, delta = carry
        query = qg_buf[:, 0].reshape(block, HEAD_DIM)
        grad = qg_buf[:, 1].reshape(block, HEAD_DIM)
        scores = lax.dot_general(kv_buf[slot, 0], query, NT, preferred_element_type=jnp.float32)
        key_held = jnp.concatenate([key_pos[slot]] * (block // HEAD_DIM), axis=1)
        scores = jnp.where(key_held <= pos_row, scores * scaling, -1e30)
        here = jnp.max(jnp.max(eights(scores), axis=0), axis=0, keepdims=True)
        new_top = jnp.maximum(top, here)
        unscaled = jnp.exp(scores - new_top)
        probs = lax.dot_general(kv_buf[slot, 1], grad, NT, preferred_element_type=jnp.float32)
        z_buf[slot] = unscaled
        p_buf[slot] = probs
        tops[slot] = jnp.broadcast_to(new_top, (8, block))
        alpha = jnp.exp(top - new_top)
        total = total * alpha + jnp.sum(eights(unscaled), axis=0)
        delta = delta * alpha + jnp.sum(eights(unscaled * probs), axis=0)
        return new_top, total, delta

    def arrive_turn(step, carry):
        j = step // ratio
        m = lax.rem(step, ratio)
        i = lax.rem(mine + heads - j, heads)

        @pl.when((m == 0) & (j > 0))
        def _():
            kv_copy(j).wait()

        @pl.when(m == 0)
        def _():
            def start_turn(other, inner):
                mate_copy(other, j).start()
                return inner

            lax.fori_loop(1, ratio, start_turn, 0)

        @pl.when(m > 0)
        def _():
            mate_copy(m, j).wait()

        return stats(lax.rem(lane + ratio - m, ratio) * heads + i, carry)

    zero = jnp.zeros((8, block), jnp.float32)
    top, total, delta = lax.fori_loop(
        0, members, arrive_turn, (jnp.full((1, block), -1e30, jnp.float32), zero, zero)
    )
    inverse = 1.0 / jnp.sum(total, axis=0, keepdims=True)
    delta = jnp.sum(delta, axis=0, keepdims=True) * inverse
    dq_acc[...] = jnp.zeros_like(dq_acc)

    def terms(slot):
        query = qg_buf[:, 0].reshape(block, HEAD_DIM)
        grad = qg_buf[:, 1].reshape(block, HEAD_DIM)
        weights = z_buf[slot] * (jnp.exp(tops[slot][0:1] - top) * inverse)
        value_term = jnp.dot(
            weights.astype(jnp.bfloat16), grad, preferred_element_type=jnp.float32
        )
        grad_scores = (weights * ((p_buf[slot] - delta) * scaling)).astype(jnp.bfloat16)
        key_term = jnp.dot(grad_scores, query, preferred_element_type=jnp.float32)
        dq_acc[...] += lax.dot_general(
            kv_buf[slot, 0], grad_scores, TN, preferred_element_type=jnp.float32
        )
        return key_term, value_term

    def part_copy(m, i):
        return pltpu.make_async_remote_copy(
            src_ref=part_stage.at[m - 1, i], dst_ref=part_mates.at[m - 1, i],
            send_sem=part_send.at[m, i], recv_sem=part_recv.at[m, i],
            device_id={"seq": mine * ratio + lax.rem(lane + m, ratio), "head": group},
            device_id_type=MESH,
        )

    def back_copy(j):
        i = lax.rem(mine + 1 + j, heads)
        return pltpu.make_async_remote_copy(
            src_ref=kv_final.at[i], dst_ref=kv_back.at[mine],
            send_sem=back_send.at[j], recv_sem=back_recv.at[j],
            device_id={"seq": i * ratio + lane, "head": group}, device_id_type=MESH,
        )

    def mate_part(m, j):
        i = lax.rem(mine + 1 + j, heads)
        key_term, value_term = terms(lax.rem(lane + m, ratio) * heads + i)
        part_stage[m - 1, i, 0] = key_term.astype(jnp.bfloat16)
        part_stage[m - 1, i, 1] = value_term.astype(jnp.bfloat16)
        part_copy(m, i).start()

    def own_part(j):
        i = lax.rem(mine + 1 + j, heads)
        key_term, value_term = terms(lane * heads + i)
        for m in range(1, ratio):
            part_copy(m, i).wait()
            key_term = key_term + part_mates[m - 1, i, 0].astype(jnp.float32)
            value_term = value_term + part_mates[m - 1, i, 1].astype(jnp.float32)
        kv_final[i, 0] = key_term.astype(jnp.bfloat16)
        kv_final[i, 1] = value_term.astype(jnp.bfloat16)

        @pl.when(j < heads - 1)
        def _():
            back_copy(j).start()

    def grads_turn(j, carry):
        @pl.when(j < heads)
        def _():
            def mate_turn(m, inner):
                mate_part(m, j)
                return inner

            lax.fori_loop(1, ratio, mate_turn, 0)

        @pl.when(j > 0)
        def _():
            own_part(j - 1)

        return carry

    lax.fori_loop(0, heads + 1, grads_turn, 0)
    kv_back[mine] = kv_final[mine]

    grad_query = dq_acc[...].T.astype(jnp.bfloat16)
    dq_stage[...] = grad_query.reshape(heads, groups, part_rows, HEAD_DIM)

    def dq_copy(j, e):
        i = lax.rem(mine + 1 + j, heads)
        other = lax.rem(group + e, groups)
        return pltpu.make_async_remote_copy(
            src_ref=dq_stage.at[i, other], dst_ref=dq_back.at[group * heads + mine],
            send_sem=dq_send.at[j, e], recv_sem=dq_recv.at[j, e],
            device_id={"seq": i * ratio + lane, "head": other}, device_id_type=MESH,
        )

    remote = [(j, e) for j in range(heads) for e in range(groups) if (j, e) != (heads - 1, 0)]
    for j, e in remote:
        dq_copy(j, e).start()
    dq_back[group * heads + mine] = dq_stage[mine, group]

    for j in range(heads - 1):
        back_copy(j).wait()
    for h in range(heads):
        dk_out[:, h * HEAD_DIM:(h + 1) * HEAD_DIM] = kv_back[h, 0]
        dv_out[:, h * HEAD_DIM:(h + 1) * HEAD_DIM] = kv_back[h, 1]
    for j, e in remote:
        dq_copy(j, e).wait()
    for h in range(groups * heads):
        dq_out[:, h * HEAD_DIM:(h + 1) * HEAD_DIM] = dq_back[h]


def local(members, groups, query_rows, key_rows, value_rows, grad_output, positions):
    rows, wide = query_rows.shape
    heads = wide // HEAD_DIM
    ratio = members // heads
    width = -(-rows // HEAD_DIM) * HEAD_DIM
    block = heads * rows
    position_rows = jnp.broadcast_to(
        jnp.pad(positions.astype(jnp.float32), (0, width - rows))[None], (8, width)
    )
    low, full = jnp.bfloat16, jnp.float32
    piece = (rows, HEAD_DIM)
    dma = pltpu.SemaphoreType.DMA
    mates = max(ratio - 1, 1)
    scratch = [
        pltpu.VMEM((heads, 2) + piece, low),
        pltpu.VMEM((members, 2) + piece, low),
        pltpu.VMEM((heads, 2) + piece, low),
        pltpu.VMEM((heads, 2) + piece, low),
        pltpu.VMEM((members, 8, width), full),
        pltpu.VMEM((members,) + piece, full),
        pltpu.VMEM((members, 8, block), full),
        pltpu.VMEM((members, rows, block), full),
        pltpu.VMEM((members, rows, block), full),
        pltpu.VMEM((HEAD_DIM, block), full),
        pltpu.VMEM((mates, heads, 2) + piece, low),
        pltpu.VMEM((mates, heads, 2) + piece, low),
        pltpu.VMEM((heads, 2) + piece, low),
        pltpu.VMEM((heads, 2) + piece, low),
        pltpu.VMEM((heads, groups, rows // groups, HEAD_DIM), low),
        pltpu.VMEM((groups * heads, rows // groups, HEAD_DIM), low),
        dma((2, heads)), dma((2, heads)), dma((heads,)), dma((heads,)), dma((heads,)),
        dma((heads,)), dma((members,)), dma((members,)),
        dma((ratio, heads)), dma((ratio, heads)),
        dma((ratio, heads)), dma((ratio, heads)), dma((heads,)), dma((heads,)),
        dma((heads, groups)), dma((heads, groups)),
    ]
    vmem = pl.BlockSpec(memory_space=pltpu.VMEM)
    hbm = pl.BlockSpec(memory_space=pl.ANY)
    return pl.pallas_call(
        functools.partial(kernel, members, heads, groups, rows, width),
        out_shape=(
            jax.ShapeDtypeStruct((rows // groups, groups * wide), low),
            jax.ShapeDtypeStruct((rows, wide), low),
            jax.ShapeDtypeStruct((rows, wide), low),
        ),
        in_specs=[vmem, hbm, hbm, hbm, hbm],
        out_specs=(vmem, vmem, vmem),
        scratch_shapes=scratch,
        compiler_params=pltpu.CompilerParams(
            collective_id=0, has_side_effects=True, vmem_limit_bytes=63 * 1024 * 1024
        ),
    )(position_rows, query_rows, key_rows, value_rows, grad_output)


def solution(mesh):
    placed = (P("seq", "head"), P("seq", "head"), P("seq", "head"), P("seq", "head"), P("seq"))
    return jax.shard_map(
        functools.partial(local, mesh.shape["seq"], mesh.shape["head"]),
        mesh=mesh,
        in_specs=placed,
        out_specs=(P(("seq", "head"), None), P("seq", "head"), P("seq", "head")),
        check_vma=False,
    )
```

profile of v0, /device:TPU:0, one launch (start us, length us, event | category | flops | bytes accessed | tf_op | source)
XLA Modules:
  0.0 90.6 jit_solution(7067225824193640414)
XLA Ops:
  0.6 0.7 convert_element_type.5
  1.3 0.6 broadcast_in_dim.2.pos_ref
  1.9 85.0 %shard_map.76 = (bf16[96,2048]{1,0:T(8,128)(2,1)}, bf16[192,1024]{1,0:T(8,128)(2,1)}, bf16[192,1024]{1,0:T(8,128)(2,1)}) custom-call(f32[8,256]{1,0:T(8,128)} %broadcast_in_dim.2.pos_ref, bf16[192,1024]{1,0:T(8,128)(2,1)} %q_hbm.1, bf16[192,1024]{1,0:T(8,128)(2,1)} %k_hbm.1, bf16[192,1024]{1,0:T(8,128)(2,1)} %v_hbm.1, bf16[192,1024]{1,0:T(8,128)(2,1)} %g_hbm.1), custom_call_target="tpu_custom_call" | custom-call | tf_op jit(solution)/shard_map/pallas_call | solution.py:326
  86.9 0.0 copy-start.1
  86.9 1.8 %copy.11 = bf16[96,2048]{1,0:T(8,128)(2,1)} copy(bf16[96,2048]{1,0:T(8,128)(2,1)} %get-tuple-element.6) | data formatting | bytes 786432
  88.8 0.0 copy-done.1
  88.8 0.0 copy-start
  88.8 0.7 copy.12
  89.5 0.4 copy-done
  89.9 0.7 copy.13
  (1 shorter events, 0.0 us)
Async XLA Ops:
  86.9 1.8 %copy-start.1 = (bf16[192,1024]{1,0:T(8,128)(2,1)S(1)}, bf16[192,1024]{1,0:T(8,128)(2,1)}, u32[]{:S(2)}) copy-start(bf16[192,1024]{1,0:T(8,128)(2,1)} %get-tuple-element.7) | copy-start | bytes 1179652
  88.8 1.1 %copy-start = (bf16[192,1024]{1,0:T(8,128)(2,1)S(1)}, bf16[192,1024]{1,0:T(8,128)(2,1)}, u32[]{:S(2)}) copy-start(bf16[192,1024]{1,0:T(8,128)(2,1)} %get-tuple-element.8) | copy-start | bytes 1179652
where the time goes:
time: 91.8 us; the launch traced here: 90.6 us
  Pallas kernels  85 us (93%)
  local copies, waits for them, and re-layouts  4.31 us (5%)
    pallas_call x1, Pallas kernels, local(): pl.pallas_call(functools.partial(kernel, members, heads, groups, rows, wi...  85 us
    unnamed x7, local copies, waits for them, and re-layouts  3.7 us

commit v1 on v0

v1 whole, which is shorter than its diff:
```python
import functools
import math

import jax
import jax.numpy as jnp
from jax import lax
from jax.experimental import pallas as pl
from jax.experimental.pallas import tpu as pltpu
from jax.sharding import PartitionSpec as P

HEAD_DIM = 128
MESH = pl.DeviceIdType.MESH
NT = (((1,), (1,)), ((), ()))
LOW = -1e30


def kernel(
    members, heads, groups, rows, width, pair, step,
    pos_ref, q_hbm, k_hbm, v_hbm, g_hbm,
    dq_out, dk_out, dv_out,
    qg_buf, kv_buf, qg_stage, kv_stage, key_t, pos_mine, pos_buf, key_pos, tops,
    z_buf, p_buf, dk_acc, dv_acc, stat_buf, kv_final, kv_back, dq_stage, dq_back,
    qg_local, kv_local, qg_send, qg_recv, kv_send, kv_recv, pos_send, pos_recv,
    stat_send, stat_recv, back_send, back_recv, dq_send, dq_recv,
):
    ratio = members // heads
    units = members // pair
    wide = heads // pair
    me = lax.axis_index("seq")
    group = lax.axis_index("head")
    mine = lax.rem(me, heads)
    mates = me // heads
    place = mine // pair
    core = lax.rem(mine, pair)
    scaling = HEAD_DIM ** (-0.5)
    sharp = scaling / math.log(2.0)
    block = pair * rows
    keys = heads * rows
    steps = heads // step
    part_rows = rows // groups

    def columns(index):
        return pl.ds(pl.multiple_of(index * HEAD_DIM, HEAD_DIM), HEAD_DIM)

    kv_order = [lax.rem(mine + j, heads) for j in range(heads)]

    def target(t, c):
        return lax.rem(place + wide - t, wide) * pair + lax.rem(core + c, pair)

    near = [(t, c) for t in range(wide) for c in range(pair)]

    def local_copies(arrays, index, first, stage, sems, j):
        return [
            pltpu.make_async_copy(
                array.at[:, columns(index)], first.at[a] if j == 0 else stage.at[j, a],
                sems.at[a, j],
            )
            for a, array in enumerate(arrays)
        ]

    kv_locals = [
        local_copies((k_hbm, v_hbm), kv_order[j], kv_buf.at[mine], kv_stage, kv_local, j)
        for j in range(heads)
    ]
    qg_locals = [
        local_copies((q_hbm, g_hbm), target(t, c), qg_buf.at[me], qg_stage, qg_local, j)
        for j, (t, c) in enumerate(near)
    ]
    for copies in kv_locals[1:] + qg_locals + kv_locals[:1]:
        for copy in copies:
            copy.start()

    pos_mine[...] = pos_ref[...]
    barrier = pltpu.get_barrier_semaphore()
    for d in range(members):
        for e in range(groups):
            if d or e:
                pl.semaphore_signal(
                    barrier, inc=1,
                    device_id={
                        "seq": lax.rem(me + d, members), "head": lax.rem(group + e, groups),
                    },
                    device_id_type=MESH,
                )
    pl.semaphore_wait(barrier, members * groups - 1)

    def remote(source, sink, send, recv, seq, head):
        return pltpu.make_async_remote_copy(
            src_ref=source, dst_ref=sink, send_sem=send, recv_sem=recv,
            device_id={"seq": seq, "head": head}, device_id_type=MESH,
        )

    def pos_copy(d, origin):
        return remote(
            pos_mine, pos_buf.at[origin], pos_send.at[d], pos_recv.at[origin],
            lax.rem(me + d, members), group,
        )

    def kv_copy(j, origin):
        return remote(
            kv_stage.at[j], kv_buf.at[origin], kv_send.at[j], kv_recv.at[origin],
            mates * heads + kv_order[j], group,
        )

    def qg_copy(j, d, origin):
        source = qg_buf.at[me] if j == 0 else qg_stage.at[j]
        return remote(
            source, qg_buf.at[origin], qg_send.at[j, d], qg_recv.at[origin],
            lax.rem(mates + d, ratio) * heads + target(*near[j]), group,
        )

    for d in range(1, members):
        pos_copy(d, me).start()
    for j in range(1, heads):
        for copy in kv_locals[j]:
            copy.wait()
        kv_copy(j, mine).start()
    for j in range(heads):
        for copy in qg_locals[j]:
            copy.wait()
        for d in range(ratio):
            if j or d:
                qg_copy(j, d, me).start()

    dk_acc[...] = jnp.zeros_like(dk_acc)
    dv_acc[...] = jnp.zeros_like(dv_acc)
    pos_buf[me] = pos_mine[...]
    for d in range(1, members):
        pos_copy(d, lax.rem(me + members - d, members)).wait()

    def spread(i, carry):
        row = jnp.broadcast_to(
            pos_buf[mates * heads + i].astype(jnp.float32), (HEAD_DIM, width)
        )
        key_pos[i] = row.T[:rows]
        return carry

    lax.fori_loop(0, heads, spread, 0)
    for copy in kv_locals[0]:
        copy.wait()
    for j in range(1, heads):
        kv_copy(j, lax.rem(mine + heads - j, heads)).wait()

    def turn(i, carry):
        held = kv_buf[i, 0].astype(jnp.float32)
        key_t[i] = held.T.astype(jnp.bfloat16)
        return carry

    lax.fori_loop(0, heads, turn, 0)

    def unit_of(n):
        d = lax.rem(n, ratio)
        t = n // ratio
        return lax.rem(mates + d, ratio) * wide + lax.rem(place + t, wide)

    def operand(unit, a):
        return qg_buf[pl.ds(unit * pair, pair), a].reshape(block, HEAD_DIM)

    def tiles(values):
        return values.reshape(step * rows // 8, 8, block)

    def stat_copy(unit, d, origin):
        return remote(
            stat_buf.at[mates, unit], stat_buf.at[origin, unit],
            stat_send.at[d, unit], stat_recv.at[origin, unit],
            lax.rem(mates + d, ratio) * heads + mine, group,
        )

    def stats(n, outer):
        unit = unit_of(n)
        for c in range(pair):
            origin = unit * pair + c

            @pl.when(origin != me)
            def _():
                remote(
                    qg_buf.at[origin], qg_buf.at[origin], qg_send.at[0, 0], qg_recv.at[origin],
                    me, group,
                ).wait_recv()

        query, grad = operand(unit, 0), operand(unit, 1)
        rows_of = [pos_buf[unit * pair + c].astype(jnp.float32)[:, :rows] for c in range(pair)]
        pos_row = jnp.concatenate(rows_of, axis=1) if pair > 1 else rows_of[0]

        def one(s, carry):
            top, total, delta = carry
            held = pl.ds(s * step, step)
            key = kv_buf[held, 0].reshape(step * rows, HEAD_DIM)
            value = kv_buf[held, 1].reshape(step * rows, HEAD_DIM)
            scores = lax.dot_general(key, query, NT, preferred_element_type=jnp.float32)
            key_held = key_pos[held].reshape(step * rows, HEAD_DIM)
            key_held = jnp.concatenate([key_held] * (block // HEAD_DIM), axis=1)
            scores = jnp.where(key_held <= pos_row, scores, LOW)
            here = jnp.max(jnp.max(tiles(scores), axis=0), axis=0, keepdims=True)
            new_top = jnp.maximum(top, here)
            unscaled = jnp.exp2((scores - new_top) * sharp)
            probs = lax.dot_general(value, grad, NT, preferred_element_type=jnp.float32)
            z_buf[n, s] = unscaled
            p_buf[n, s] = probs
            tops[n, s] = jnp.broadcast_to(new_top, (8, block))
            alpha = jnp.exp2((top - new_top) * sharp)
            total = total * alpha + jnp.sum(tiles(unscaled), axis=0)
            delta = delta * alpha + jnp.sum(tiles(unscaled * probs), axis=0)
            return new_top, total, delta

        zero = jnp.zeros((8, block), jnp.float32)
        top, total, delta = lax.fori_loop(
            0, steps, one, (jnp.full((1, block), LOW, jnp.float32), zero, zero)
        )
        total = jnp.sum(total, axis=0, keepdims=True)
        delta = jnp.sum(delta, axis=0, keepdims=True)
        stat_buf[mates, unit] = jnp.concatenate(
            [top, total, delta, jnp.zeros((5, block), jnp.float32)], axis=0
        )
        for d in range(1, ratio):
            stat_copy(unit, d, mates).start()
        return outer

    lax.fori_loop(0, units, stats, 0)

    def grads(n, outer):
        unit = unit_of(n)
        for d in range(1, ratio):
            stat_copy(unit, d, lax.rem(mates + ratio - d, ratio)).wait()
        whole = [stat_buf[d, unit] for d in range(ratio)]
        top = functools.reduce(jnp.maximum, [w[0:1] for w in whole])
        shares = [jnp.exp2((w[0:1] - top) * sharp) for w in whole]
        inverse = 1.0 / functools.reduce(jnp.add, [w[1:2] * s for w, s in zip(whole, shares)])
        delta = functools.reduce(jnp.add, [w[2:3] * s for w, s in zip(whole, shares)]) * inverse
        query, grad = operand(unit, 0), operand(unit, 1)

        def one(s, query_t):
            held = pl.ds(s * step, step)
            factor = jnp.exp2((tops[n, s][0:1] - top) * sharp) * inverse
            weights = z_buf[n, s] * factor
            grad_scores = (weights * (p_buf[n, s] - delta)).astype(jnp.bfloat16)
            value_term = jnp.dot(
                weights.astype(jnp.bfloat16), grad, preferred_element_type=jnp.float32
            )
            key_term = jnp.dot(grad_scores, query, preferred_element_type=jnp.float32)
            dv_acc[held] += value_term.reshape(step, rows, HEAD_DIM)
            dk_acc[held] += key_term.reshape(step, rows, HEAD_DIM)
            for i in range(step):
                query_t = query_t + jnp.dot(
                    key_t[s * step + i], grad_scores[i * rows:(i + 1) * rows],
                    preferred_element_type=jnp.float32,
                )
            return query_t

        query_t = lax.fori_loop(0, steps, one, jnp.zeros((HEAD_DIM, block), jnp.float32))
        grad_query = (query_t * scaling).T.astype(jnp.bfloat16)
        grad_query = grad_query.reshape(pair, groups, part_rows, HEAD_DIM)
        dq_stage[unit] = grad_query
        for c in range(pair):
            for e in range(groups):
                owner = unit * pair + c
                other = lax.rem(group + e, groups)
                copy = remote(
                    dq_stage.at[unit, c, other], dq_back.at[mates, group * heads + mine],
                    dq_send.at[unit, c, e], dq_recv.at[mates, group * heads + mine],
                    owner, other,
                )
                if e:
                    copy.start()
                else:
                    pl.when(owner != me)(copy.start)
        return outer

    lax.fori_loop(0, units, grads, 0)

    dq_back[mates, group * heads + mine] = dq_stage[me // pair, core, group]

    def back_copy(j, origin):
        return remote(
            kv_final.at[j], kv_back.at[origin], back_send.at[j], back_recv.at[origin],
            mates * heads + kv_order[j], group,
        )

    for j in range(1, heads):
        kv_final[j, 0] = (dk_acc[kv_order[j]] * scaling).astype(jnp.bfloat16)
        kv_final[j, 1] = dv_acc[kv_order[j]].astype(jnp.bfloat16)
        back_copy(j, mine).start()
    kv_back[mine, 0] = (dk_acc[mine] * scaling).astype(jnp.bfloat16)
    kv_back[mine, 1] = dv_acc[mine].astype(jnp.bfloat16)

    for j in range(heads):
        for d in range(ratio):
            if j or d:
                qg_copy(j, d, me).wait_send()

    def dq_sent(unit, outer):
        for c in range(pair):
            for e in range(groups):
                owner = unit * pair + c
                other = lax.rem(group + e, groups)
                copy = remote(
                    dq_stage.at[unit, c, other], dq_back.at[mates, group * heads + mine],
                    dq_send.at[unit, c, e], dq_recv.at[mates, group * heads + mine],
                    owner, other,
                )
                if e:
                    copy.wait_send()
                else:
                    pl.when(owner != me)(copy.wait_send)
        return outer

    lax.fori_loop(0, units, dq_sent, 0)

    for d in range(ratio):
        for e in range(groups):
            for i in range(heads):
                giver = lax.rem(mates + d, ratio)
                slot = lax.rem(group + e, groups) * heads + lax.rem(mine + i, heads)
                if d or e or i:
                    remote(
                        dq_back.at[giver, slot], dq_back.at[giver, slot],
                        dq_send.at[0, 0, 0], dq_recv.at[giver, slot], me, group,
                    ).wait_recv()
    for h in range(groups * heads):
        parts = [dq_back[d, h].astype(jnp.float32) for d in range(ratio)]
        dq_out[:, h * HEAD_DIM:(h + 1) * HEAD_DIM] = functools.reduce(jnp.add, parts).astype(
            jnp.bfloat16
        )
    for j in range(1, heads):
        back_copy(j, lax.rem(mine + heads - j, heads)).wait()
    for h in range(heads):
        dk_out[:, h * HEAD_DIM:(h + 1) * HEAD_DIM] = kv_back[h, 0]
        dv_out[:, h * HEAD_DIM:(h + 1) * HEAD_DIM] = kv_back[h, 1]


def local(members, groups, query_rows, key_rows, value_rows, grad_output, positions):
    rows, wide = query_rows.shape
    heads = wide // HEAD_DIM
    ratio = members // heads
    width = -(-rows // HEAD_DIM) * HEAD_DIM
    pair = HEAD_DIM // math.gcd(rows, HEAD_DIM)
    step = math.gcd(heads, 2)
    units = members // pair
    block = pair * rows
    keys = heads * rows
    position_rows = jnp.pad(positions, (0, width - rows))[None]
    low, full = jnp.bfloat16, jnp.float32
    piece = (rows, HEAD_DIM)
    dma = pltpu.SemaphoreType.DMA
    scratch = [
        pltpu.VMEM((members, 2) + piece, low),
        pltpu.VMEM((heads, 2) + piece, low),
        pltpu.VMEM((heads, 2) + piece, low),
        pltpu.VMEM((heads, 2) + piece, low),
        pltpu.VMEM((heads, HEAD_DIM, rows), low),
        pltpu.VMEM((1, width), jnp.int32),
        pltpu.VMEM((members, 1, width), jnp.int32),
        pltpu.VMEM((heads,) + piece, full),
        pltpu.VMEM((units, heads // step, 8, block), full),
        pltpu.VMEM((units, heads // step, step * rows, block), full),
        pltpu.VMEM((units, heads // step, step * rows, block), full),
        pltpu.VMEM((heads,) + piece, full),
        pltpu.VMEM((heads,) + piece, full),
        pltpu.VMEM((ratio, units, 8, block), full),
        pltpu.VMEM((heads, 2) + piece, low),
        pltpu.VMEM((heads, 2) + piece, low),
        pltpu.VMEM((units, pair, groups, rows // groups, HEAD_DIM), low),
        pltpu.VMEM((ratio, groups * heads, rows // groups, HEAD_DIM), low),
        dma((2, heads)), dma((2, heads)), dma((heads, ratio)), dma((members,)),
        dma((heads,)), dma((heads,)), dma((members,)), dma((members,)),
        dma((ratio, units)), dma((ratio, units)), dma((heads,)), dma((heads,)),
        dma((units, pair, groups)), dma((ratio, groups * heads)),
    ]
    vmem = pl.BlockSpec(memory_space=pltpu.VMEM)
    hbm = pl.BlockSpec(memory_space=pl.ANY)
    return pl.pallas_call(
        functools.partial(kernel, members, heads, groups, rows, width, pair, step),
        out_shape=(
            jax.ShapeDtypeStruct((rows // groups, groups * wide), low),
            jax.ShapeDtypeStruct((rows, wide), low),
            jax.ShapeDtypeStruct((rows, wide), low),
        ),
        in_specs=[vmem, hbm, hbm, hbm, hbm],
        out_specs=(vmem, vmem, vmem),
        scratch_shapes=scratch,
        compiler_params=pltpu.CompilerParams(
            collective_id=0, has_side_effects=True, vmem_limit_bytes=63 * 1024 * 1024
        ),
    )(position_rows, query_rows, key_rows, value_rows, grad_output)


def solution(mesh):
    placed = (P("seq", "head"), P("seq", "head"), P("seq", "head"), P("seq", "head"), P("seq"))
    return jax.shard_map(
        functools.partial(local, mesh.shape["seq"], mesh.shape["head"]),
        mesh=mesh,
        in_specs=placed,
        out_specs=(P(("seq", "head"), None), P("seq", "head"), P("seq", "head")),
        check_vma=False,
    )
```

time: 91.8 us -> 85.2 us (0.928); the launches traced: 90.6 us -> 85 us
  Pallas kernels: 85 us -> 79.4 us
    pallas_call x1, Pallas kernels: 85 us -> 79.4 us  [local(): pl.pallas_call(functools.partial(kernel, members, heads, groups, rows, wi...]
    pad x1, local copies, waits for them, and re-layouts: 0.01 us -> 1.24 us  [local(): position_rows = jnp.pad(positions, (0, width - rows))[None]]
where the time goes in v1:
time: 85.2 us; the launch traced here: 85 us
  Pallas kernels  79.4 us (93%)
  local copies, waits for them, and re-layouts  4.95 us (6%)
    pallas_call x1, Pallas kernels, local(): pl.pallas_call(functools.partial(kernel, members, heads, groups, rows, wi...  79.4 us
    unnamed x7, local copies, waits for them, and re-layouts  3.7 us

profile of v1, /device:TPU:0, one launch (start us, length us, event | category | flops | bytes accessed | tf_op | source)
XLA Modules:
  0.0 85.0 jit_solution(15144686757017550626)
XLA Ops:
  0.6 1.2 %pad.4 = s32[256]{0:T(256)} pad(s32[192]{0:T(256)} %param.9, s32[]{:T(128)} %constant.0.clone.1), padding=0_64 | pad | bytes 1796 | tf_op jit(solution)/shard_map/jit(_pad)/pad | solution.py:341
  1.9 79.4 %shard_map.76 = (bf16[96,2048]{1,0:T(8,128)(2,1)}, bf16[192,1024]{1,0:T(8,128)(2,1)}, bf16[192,1024]{1,0:T(8,128)(2,1)}) custom-call(s32[1,256]{1,0:T(1,128)} %bitcast.1, bf16[192,1024]{1,0:T(8,128)(2,1)} %q_hbm.1, bf16[192,1024]{1,0:T(8,128)(2,1)} %k_hbm.1, bf16[192,1024]{1,0:T(8,128)(2,1)} %v_hbm.1, bf16[192,1024]{1,0:T(8,128)(2,1)} %g_hbm.1), custom_call_target="tpu_custom_call" | custom-call | tf_op jit(solution)/shard_map/pallas_call | solution.py:371
  81.2 0.0 copy-start.1
  81.3 1.8 %copy.11 = bf16[96,2048]{1,0:T(8,128)(2,1)} copy(bf16[96,2048]{1,0:T(8,128)(2,1)} %get-tuple-element.6) | data formatting | bytes 786432
  83.1 0.0 copy-done.1
  83.1 0.0 copy-start
  83.1 0.7 copy.12
  83.8 0.4 copy-done
  84.2 0.7 copy.13
Async XLA Ops:
  81.2 1.8 %copy-start.1 = (bf16[192,1024]{1,0:T(8,128)(2,1)S(1)}, bf16[192,1024]{1,0:T(8,128)(2,1)}, u32[]{:S(2)}) copy-start(bf16[192,1024]{1,0:T(8,128)(2,1)} %get-tuple-element.7) | copy-start | bytes 1179652
  83.1 1.1 %copy-start = (bf16[192,1024]{1,0:T(8,128)(2,1)S(1)}, bf16[192,1024]{1,0:T(8,128)(2,1)}, u32[]{:S(2)}) copy-start(bf16[192,1024]{1,0:T(8,128)(2,1)} %get-tuple-element.8) | copy-start | bytes 1179652

commit v2 on v1

--- a/solution.py
+++ b/solution.py
@@ -12,6 +12,22 @@
 MESH = pl.DeviceIdType.MESH
 NT = (((1,), (1,)), ((), ()))
 LOW = -1e30
+PAIR = 2
+STEP = 4
+SEND_OUTER, SEND_INNER = "kCRh", "kCRh"
+STATS_OUTER, STATS_INNER = "CRh", "CRh"
+GRADS_OUTER, GRADS_INNER = "HCR", "RCH"
+BACK_OUTER, BACK_INNER = "rC", "Cr"
+
+
+def walk(order, sizes):
+    found = [{}]
+    for axis in order:
+        values = list(range(sizes[axis.lower()]))
+        if axis.isupper():
+            values.reverse()
+        found = [{**one, axis.lower(): v} for one in found for v in values]
+    return found
 
 
 def kernel(
@@ -26,51 +42,66 @@
     ratio = members // heads
     units = members // pair
     wide = heads // pair
+    lines = 2 if wide % 2 == 0 else 1
+    across = wide // lines
+    sizes = {"h": ratio, "r": lines, "c": across, "k": 2}
     me = lax.axis_index("seq")
     group = lax.axis_index("head")
     mine = lax.rem(me, heads)
     mates = me // heads
     place = mine // pair
     core = lax.rem(mine, pair)
+    line = place // across
+    column = lax.rem(place, across)
+    outer = (2 * mates < ratio) == (2 * line < lines)
     scaling = HEAD_DIM ** (-0.5)
     sharp = scaling / math.log(2.0)
     block = pair * rows
-    keys = heads * rows
     steps = heads // step
     part_rows = rows // groups
 
+    def by_row(act_outer, act_inner):
+        pl.when(outer)(act_outer)
+        pl.when(jnp.logical_not(outer))(act_inner)
+
     def columns(index):
         return pl.ds(pl.multiple_of(index * HEAD_DIM, HEAD_DIM), HEAD_DIM)
 
-    kv_order = [lax.rem(mine + j, heads) for j in range(heads)]
-
-    def target(t, c):
-        return lax.rem(place + wide - t, wide) * pair + lax.rem(core + c, pair)
-
-    near = [(t, c) for t in range(wide) for c in range(pair)]
-
-    def local_copies(arrays, index, first, stage, sems, j):
+    others = [(r, c, e) for r in range(lines) for c in range(across) for e in range(pair)]
+
+    def place_of(r, c):
+        return lax.rem(line + r, lines) * across + lax.rem(column + c, across)
+
+    def ahead(j):
+        r, c, e = others[j]
+        return place_of(r, c) * pair + lax.rem(core + e, pair)
+
+    def behind(j):
+        r, c, e = others[j]
+        return place_of(lines - r, across - c) * pair + lax.rem(core + pair - e, pair)
+
+    def local_copies(arrays, first, stage, sems, j):
         return [
             pltpu.make_async_copy(
-                array.at[:, columns(index)], first.at[a] if j == 0 else stage.at[j, a],
+                array.at[:, columns(ahead(j))], first.at[a] if j == 0 else stage.at[j, a],
                 sems.at[a, j],
             )
             for a, array in enumerate(arrays)
         ]
 
     kv_locals = [
-        local_copies((k_hbm, v_hbm), kv_order[j], kv_buf.at[mine], kv_stage, kv_local, j)
+        local_copies((k_hbm, v_hbm), kv_buf.at[mine], kv_stage, kv_local, j)
         for j in range(heads)
     ]
     qg_locals = [
-        local_copies((q_hbm, g_hbm), target(t, c), qg_buf.at[me], qg_stage, qg_local, j)
-        for j, (t, c) in enumerate(near)
+        local_copies((q_hbm, g_hbm), qg_buf.at[me], qg_stage, qg_local, j) for j in range(heads)
     ]
-    for copies in kv_locals[1:] + qg_locals + kv_locals[:1]:
+    for copies in kv_locals + qg_locals:
         for copy in copies:
             copy.start()
 
-    pos_mine[...] = pos_ref[...]
+    pos_mine[...] = jnp.zeros_like(pos_mine)
+    pos_mine[:, :rows] = pos_ref[...]
     barrier = pltpu.get_barrier_semaphore()
     for d in range(members):
         for e in range(groups):
@@ -99,28 +130,35 @@
     def kv_copy(j, origin):
         return remote(
             kv_stage.at[j], kv_buf.at[origin], kv_send.at[j], kv_recv.at[origin],
-            mates * heads + kv_order[j], group,
-        )
-
-    def qg_copy(j, d, origin):
+            mates * heads + ahead(j), group,
+        )
+
+    def qg_copy(j, d):
         source = qg_buf.at[me] if j == 0 else qg_stage.at[j]
         return remote(
-            source, qg_buf.at[origin], qg_send.at[j, d], qg_recv.at[origin],
-            lax.rem(mates + d, ratio) * heads + target(*near[j]), group,
-        )
-
+            source, qg_buf.at[me], qg_send.at[j, d], qg_recv.at[me],
+            lax.rem(mates + d, ratio) * heads + ahead(j), group,
+        )
+
+    for copies in kv_locals + qg_locals:
+        for copy in copies:
+            copy.wait()
     for d in range(1, members):
         pos_copy(d, me).start()
-    for j in range(1, heads):
-        for copy in kv_locals[j]:
-            copy.wait()
-        kv_copy(j, mine).start()
-    for j in range(heads):
-        for copy in qg_locals[j]:
-            copy.wait()
-        for d in range(ratio):
-            if j or d:
-                qg_copy(j, d, me).start()
+
+    def send_all(order):
+        def act():
+            for at in walk(order, sizes):
+                for e in range(pair):
+                    j = others.index((at["r"], at["c"], e))
+                    if at["k"] == 0 and at["h"] == 0 and j:
+                        kv_copy(j, mine).start()
+                    if at["k"] == 1 and (at["h"] or j):
+                        qg_copy(j, at["h"]).start()
+
+        return act
+
+    by_row(send_all(SEND_OUTER), send_all(SEND_INNER))
 
     dk_acc[...] = jnp.zeros_like(dk_acc)
     dv_acc[...] = jnp.zeros_like(dv_acc)
@@ -136,22 +174,30 @@
         return carry
 
     lax.fori_loop(0, heads, spread, 0)
-    for copy in kv_locals[0]:
-        copy.wait()
     for j in range(1, heads):
-        kv_copy(j, lax.rem(mine + heads - j, heads)).wait()
-
-    def turn(i, carry):
-        held = kv_buf[i, 0].astype(jnp.float32)
-        key_t[i] = held.T.astype(jnp.bfloat16)
+        kv_copy(j, behind(j)).wait()
+
+    def turn(s, carry):
+        held = kv_buf[pl.ds(s * step, step), 0].reshape(step * rows, HEAD_DIM)
+        key_t[s] = held.astype(jnp.float32).T.astype(jnp.bfloat16)
         return carry
 
-    lax.fori_loop(0, heads, turn, 0)
-
-    def unit_of(n):
-        d = lax.rem(n, ratio)
-        t = n // ratio
-        return lax.rem(mates + d, ratio) * wide + lax.rem(place + t, wide)
+    lax.fori_loop(0, steps, turn, 0)
+
+    def pick(table, k):
+        value = jnp.int32(table[0])
+        for i, entry in enumerate(table[1:]):
+            value = jnp.where(k == i + 1, entry, value)
+        return value
+
+    def unit_of(k, order_outer, order_inner):
+        tables = [
+            [(at["h"] * lines + at["r"]) * across + at["c"] for at in walk(order, sizes)]
+            for order in (order_outer, order_inner)
+        ]
+        n = jnp.where(outer, pick(tables[0], k), pick(tables[1], k))
+        there = place_of(lax.rem(n // across, lines), lax.rem(n, across))
+        return n, lax.rem(mates + n // wide, ratio) * wide + there
 
     def operand(unit, a):
         return qg_buf[pl.ds(unit * pair, pair), a].reshape(block, HEAD_DIM)
@@ -166,8 +212,8 @@
             lax.rem(mates + d, ratio) * heads + mine, group,
         )
 
-    def stats(n, outer):
-        unit = unit_of(n)
+    def stats(k, carried):
+        n, unit = unit_of(k, STATS_OUTER, STATS_INNER)
         for c in range(pair):
             origin = unit * pair + c
 
@@ -214,12 +260,12 @@
         )
         for d in range(1, ratio):
             stat_copy(unit, d, mates).start()
-        return outer
+        return carried
 
     lax.fori_loop(0, units, stats, 0)
 
-    def grads(n, outer):
-        unit = unit_of(n)
+    def grads(k, carried):
+        n, unit = unit_of(k, GRADS_OUTER, GRADS_INNER)
         for d in range(1, ratio):
             stat_copy(unit, d, lax.rem(mates + ratio - d, ratio)).wait()
         whole = [stat_buf[d, unit] for d in range(ratio)]
@@ -240,12 +286,9 @@
             key_term = jnp.dot(grad_scores, query, preferred_element_type=jnp.float32)
             dv_acc[held] += value_term.reshape(step, rows, HEAD_DIM)
             dk_acc[held] += key_term.reshape(step, rows, HEAD_DIM)
-            for i in range(step):
-                query_t = query_t + jnp.dot(
-                    key_t[s * step + i], grad_scores[i * rows:(i + 1) * rows],
-                    preferred_element_type=jnp.float32,
-                )
-            return query_t
+            return query_t + jnp.dot(
+                key_t[s], grad_scores, preferred_element_type=jnp.float32
+            )
 
         query_t = lax.fori_loop(0, steps, one, jnp.zeros((HEAD_DIM, block), jnp.float32))
         grad_query = (query_t * scaling).T.astype(jnp.bfloat16)
@@ -264,7 +307,7 @@
                     copy.start()
                 else:
                     pl.when(owner != me)(copy.start)
-        return outer
+        return carried
 
     lax.fori_loop(0, units, grads, 0)
 
@@ -273,22 +316,31 @@
     def back_copy(j, origin):
         return remote(
             kv_final.at[j], kv_back.at[origin], back_send.at[j], back_recv.at[origin],
-            mates * heads + kv_order[j], group,
-        )
-
-    for j in range(1, heads):
-        kv_final[j, 0] = (dk_acc[kv_order[j]] * scaling).astype(jnp.bfloat16)
-        kv_final[j, 1] = dv_acc[kv_order[j]].astype(jnp.bfloat16)
-        back_copy(j, mine).start()
+            mates * heads + ahead(j), group,
+        )
+
+    def give_back(order):
+        def act():
+            for at in walk(order, sizes):
+                for e in range(pair):
+                    j = others.index((at["r"], at["c"], e))
+                    if j:
+                        kv_final[j, 0] = (dk_acc[ahead(j)] * scaling).astype(jnp.bfloat16)
+                        kv_final[j, 1] = dv_acc[ahead(j)].astype(jnp.bfloat16)
+                        back_copy(j, mine).start()
+
+        return act
+
+    by_row(give_back(BACK_OUTER), give_back(BACK_INNER))
     kv_back[mine, 0] = (dk_acc[mine] * scaling).astype(jnp.bfloat16)
     kv_back[mine, 1] = dv_acc[mine].astype(jnp.bfloat16)
 
     for j in range(heads):
         for d in range(ratio):
             if j or d:
-                qg_copy(j, d, me).wait_send()
-
-    def dq_sent(unit, outer):
+                qg_copy(j, d).wait_send()
+
+    def dq_sent(unit, carried):
         for c in range(pair):
             for e in range(groups):
                 owner = unit * pair + c
@@ -302,7 +354,7 @@
                     copy.wait_send()
                 else:
                     pl.when(owner != me)(copy.wait_send)
-        return outer
+        return carried
 
     lax.fori_loop(0, units, dq_sent, 0)
 
@@ -322,7 +374,7 @@
             jnp.bfloat16
         )
     for j in range(1, heads):
-        back_copy(j, lax.rem(mine + heads - j, heads)).wait()
+        back_copy(j, behind(j)).wait()
     for h in range(heads):
         dk_out[:, h * HEAD_DIM:(h + 1) * HEAD_DIM] = kv_back[h, 0]
         dv_out[:, h * HEAD_DIM:(h + 1) * HEAD_DIM] = kv_back[h, 1]
@@ -333,12 +385,11 @@
     heads = wide // HEAD_DIM
     ratio = members // heads
     width = -(-rows // HEAD_DIM) * HEAD_DIM
-    pair = HEAD_DIM // math.gcd(rows, HEAD_DIM)
-    step = math.gcd(heads, 2)
+    pair = math.gcd(heads, PAIR)
+    step = math.gcd(heads, STEP)
     units = members // pair
     block = pair * rows
-    keys = heads * rows
-    position_rows = jnp.pad(positions, (0, width - rows))[None]
+    position_rows = positions[None]
     low, full = jnp.bfloat16, jnp.float32
     piece = (rows, HEAD_DIM)
     dma = pltpu.SemaphoreType.DMA
@@ -347,7 +398,7 @@
         pltpu.VMEM((heads, 2) + piece, low),
         pltpu.VMEM((heads, 2) + piece, low),
         pltpu.VMEM((heads, 2) + piece, low),
-        pltpu.VMEM((heads, HEAD_DIM, rows), low),
+        pltpu.VMEM((heads // step, HEAD_DIM, step * rows), low),
         pltpu.VMEM((1, width), jnp.int32),
         pltpu.VMEM((members, 1, width), jnp.int32),
         pltpu.VMEM((heads,) + piece, full),

time: 85.2 us -> 80.2 us (0.941)
  Pallas kernels: 79.4 us -> 75.6 us
  local copies, waits for them, and re-layouts: 4.95 us -> 3.7 us
    pallas_call x1, Pallas kernels: 79.4 us -> 75.6 us  [local(): pl.pallas_call(functools.partial(kernel, members, heads, groups, rows, wi...]
    pad x1 -> x0, local copies, waits for them, and re-layouts: 1.24 us -> none  [local(): position_rows = jnp.pad(positions, (0, width - rows))[None]]
where the time goes in v2:
time: 80.2 us; the launch traced here: 80 us
  Pallas kernels  75.6 us (94%)
  local copies, waits for them, and re-layouts  3.7 us (5%)
    pallas_call x1, Pallas kernels, local(): pl.pallas_call(functools.partial(kernel, members, heads, groups, rows, wi...  75.6 us
    unnamed x7, local copies, waits for them, and re-layouts  3.7 us

profile of v2, /device:TPU:0, one launch (start us, length us, event | category | flops | bytes accessed | tf_op | source)
XLA Modules:
  0.0 80.0 jit_solution(7122651144308487806)
XLA Ops:
  0.6 75.6 %shard_map.76 = (bf16[96,2048]{1,0:T(8,128)(2,1)}, bf16[192,1024]{1,0:T(8,128)(2,1)}, bf16[192,1024]{1,0:T(8,128)(2,1)}) custom-call(s32[1,192]{1,0:T(1,128)} %bitcast.1, bf16[192,1024]{1,0:T(8,128)(2,1)} %q_hbm.1, bf16[192,1024]{1,0:T(8,128)(2,1)} %k_hbm.1, bf16[192,1024]{1,0:T(8,128)(2,1)} %v_hbm.1, bf16[192,1024]{1,0:T(8,128)(2,1)} %g_hbm.1), custom_call_target="tpu_custom_call" | custom-call | tf_op jit(solution)/shard_map/pallas_call | solution.py:422
  76.2 0.0 copy-start.1
  76.3 1.8 %copy.11 = bf16[96,2048]{1,0:T(8,128)(2,1)} copy(bf16[96,2048]{1,0:T(8,128)(2,1)} %get-tuple-element.6) | data formatting | bytes 786432
  78.1 0.0 copy-done.1
  78.1 0.0 copy-start
  78.1 0.7 copy.12
  78.8 0.4 copy-done
  79.2 0.7 copy.13
Async XLA Ops:
  76.2 1.8 %copy-start.1 = (bf16[192,1024]{1,0:T(8,128)(2,1)S(1)}, bf16[192,1024]{1,0:T(8,128)(2,1)}, u32[]{:S(2)}) copy-start(bf16[192,1024]{1,0:T(8,128)(2,1)} %get-tuple-element.7) | copy-start | bytes 1179652
  78.1 1.1 %copy-start = (bf16[192,1024]{1,0:T(8,128)(2,1)S(1)}, bf16[192,1024]{1,0:T(8,128)(2,1)}, u32[]{:S(2)}) copy-start(bf16[192,1024]{1,0:T(8,128)(2,1)} %get-tuple-element.8) | copy-start | bytes 1179652

commit v3 on v2

--- a/solution.py
+++ b/solution.py
@@ -35,9 +35,9 @@
     pos_ref, q_hbm, k_hbm, v_hbm, g_hbm,
     dq_out, dk_out, dv_out,
     qg_buf, kv_buf, qg_stage, kv_stage, key_t, pos_mine, pos_buf, key_pos, tops,
-    z_buf, p_buf, dk_acc, dv_acc, stat_buf, kv_final, kv_back, dq_stage, dq_back,
+    z_buf, p_buf, dk_acc, dv_acc, stat_buf, kv_final, dq_stage, dq_back, dq_sum,
     qg_local, kv_local, qg_send, qg_recv, kv_send, kv_recv, pos_send, pos_recv,
-    stat_send, stat_recv, back_send, back_recv, dq_send, dq_recv,
+    stat_send, stat_recv, back_send, back_recv, back_own, dq_send, dq_recv, dq_own,
 ):
     ratio = members // heads
     units = members // pair
@@ -313,11 +313,18 @@
 
     dq_back[mates, group * heads + mine] = dq_stage[me // pair, core, group]
 
-    def back_copy(j, origin):
-        return remote(
-            kv_final.at[j], kv_back.at[origin], back_send.at[j], back_recv.at[origin],
-            mates * heads + ahead(j), group,
-        )
+    def back_copies(j, origin):
+        return [
+            remote(
+                kv_final.at[j, a], out.at[:, columns(origin)], back_send.at[a, j],
+                back_recv.at[a, origin], mates * heads + ahead(j), group,
+            )
+            for a, out in enumerate((dk_out, dv_out))
+        ]
+
+    def finish(j):
+        kv_final[j, 0] = (dk_acc[ahead(j)] * scaling).astype(jnp.bfloat16)
+        kv_final[j, 1] = dv_acc[ahead(j)].astype(jnp.bfloat16)
 
     def give_back(order):
         def act():
@@ -325,15 +332,20 @@
                 for e in range(pair):
                     j = others.index((at["r"], at["c"], e))
                     if j:
-                        kv_final[j, 0] = (dk_acc[ahead(j)] * scaling).astype(jnp.bfloat16)
-                        kv_final[j, 1] = dv_acc[ahead(j)].astype(jnp.bfloat16)
-                        back_copy(j, mine).start()
+                        finish(j)
+                        for copy in back_copies(j, mine):
+                            copy.start()
 
         return act
 
     by_row(give_back(BACK_OUTER), give_back(BACK_INNER))
-    kv_back[mine, 0] = (dk_acc[mine] * scaling).astype(jnp.bfloat16)
-    kv_back[mine, 1] = dv_acc[mine].astype(jnp.bfloat16)
+    finish(0)
+    back_locals = [
+        pltpu.make_async_copy(kv_final.at[0, a], out.at[:, columns(mine)], back_own.at[a])
+        for a, out in enumerate((dk_out, dv_out))
+    ]
+    for copy in back_locals:
+        copy.start()
 
     for j in range(heads):
         for d in range(ratio):
@@ -370,14 +382,34 @@
                     ).wait_recv()
     for h in range(groups * heads):
         parts = [dq_back[d, h].astype(jnp.float32) for d in range(ratio)]
-        dq_out[:, h * HEAD_DIM:(h + 1) * HEAD_DIM] = functools.reduce(jnp.add, parts).astype(
+        dq_sum[:, h * HEAD_DIM:(h + 1) * HEAD_DIM] = functools.reduce(jnp.add, parts).astype(
             jnp.bfloat16
         )
+    dq_local = pltpu.make_async_copy(dq_sum, dq_out, dq_own)
+    dq_local.start()
     for j in range(1, heads):
-        back_copy(j, behind(j)).wait()
-    for h in range(heads):
-        dk_out[:, h * HEAD_DIM:(h + 1) * HEAD_DIM] = kv_back[h, 0]
-        dv_out[:, h * HEAD_DIM:(h + 1) * HEAD_DIM] = kv_back[h, 1]
+        for copy in back_copies(j, behind(j)):
+            copy.wait()
+    for copy in back_locals + [dq_local]:
+        copy.wait()
+
+
+def settle(a_in, b_in, c_in, a_out, b_out, c_out, a_mid, b_mid, c_mid, come, go):
+    ins = [
+        pltpu.make_async_copy(source, middle, come.at[i])
+        for i, (source, middle) in enumerate(((a_in, a_mid), (b_in, b_mid), (c_in, c_mid)))
+    ]
+    outs = [
+        pltpu.make_async_copy(middle, sink, go.at[i])
+        for i, (middle, sink) in enumerate(((a_mid, a_out), (b_mid, b_out), (c_mid, c_out)))
+    ]
+    for copy in ins:
+        copy.start()
+    for copy, then in zip(ins, outs):
+        copy.wait()
+        then.start()
+    for copy in outs:
+        copy.wait()
 
 
 def local(members, groups, query_rows, key_rows, value_rows, grad_output, positions):
@@ -409,17 +441,17 @@
         pltpu.VMEM((heads,) + piece, full),
         pltpu.VMEM((ratio, units, 8, block), full),
         pltpu.VMEM((heads, 2) + piece, low),
-        pltpu.VMEM((heads, 2) + piece, low),
         pltpu.VMEM((units, pair, groups, rows // groups, HEAD_DIM), low),
         pltpu.VMEM((ratio, groups * heads, rows // groups, HEAD_DIM), low),
+        pltpu.VMEM((rows // groups, groups * wide), low),
         dma((2, heads)), dma((2, heads)), dma((heads, ratio)), dma((members,)),
         dma((heads,)), dma((heads,)), dma((members,)), dma((members,)),
-        dma((ratio, units)), dma((ratio, units)), dma((heads,)), dma((heads,)),
-        dma((units, pair, groups)), dma((ratio, groups * heads)),
+        dma((ratio, units)), dma((ratio, units)), dma((2, heads)), dma((2, heads)), dma((2,)),
+        dma((units, pair, groups)), dma((ratio, groups * heads)), dma,
     ]
     vmem = pl.BlockSpec(memory_space=pltpu.VMEM)
     hbm = pl.BlockSpec(memory_space=pl.ANY)
-    return pl.pallas_call(
+    results = pl.pallas_call(
         functools.partial(kernel, members, heads, groups, rows, width, pair, step),
         out_shape=(
             jax.ShapeDtypeStruct((rows // groups, groups * wide), low),
@@ -427,12 +459,19 @@
             jax.ShapeDtypeStruct((rows, wide), low),
         ),
         in_specs=[vmem, hbm, hbm, hbm, hbm],
-        out_specs=(vmem, vmem, vmem),
+        out_specs=(hbm, hbm, hbm),
         scratch_shapes=scratch,
         compiler_params=pltpu.CompilerParams(
             collective_id=0, has_side_effects=True, vmem_limit_bytes=63 * 1024 * 1024
         ),
     )(position_rows, query_rows, key_rows, value_rows, grad_output)
+    return pl.pallas_call(
+        settle,
+        out_shape=tuple(jax.ShapeDtypeStruct(r.shape, r.dtype) for r in results),
+        in_specs=[hbm, hbm, hbm],
+        out_specs=(hbm, hbm, hbm),
+        scratch_shapes=[pltpu.VMEM(r.shape, r.dtype) for r in results] + [dma((3,)), dma((3,))],
+    )(*results)
 
 
 def solution(mesh):

time: 80.2 us -> 77.6 us (0.968)
  local copies, waits for them, and re-layouts: 3.7 us -> 0 us
  Pallas kernels: 75.6 us -> 76.7 us
    unnamed x7 -> x0, local copies, waits for them, and re-layouts: 3.7 us -> none
    pallas_call x0 -> x1, Pallas kernels: none -> 2.05 us  [local(): pl.pallas_call(settle, out_shape=tuple((jax.ShapeDtypeStruct(r.shape, r.d...]
    pallas_call x1, Pallas kernels: 75.6 us -> 74.7 us  [local(): pl.pallas_call(functools.partial(kernel, members, heads, groups, rows, wi...]
where the time goes in v3:
time: 77.6 us; the launch traced here: 77.4 us
  Pallas kernels  76.7 us (99%)
    pallas_call x1, Pallas kernels, local(): pl.pallas_call(functools.partial(kernel, members, heads, groups, rows, wi...  74.7 us
    pallas_call x1, Pallas kernels, local(): pl.pallas_call(settle, out_shape=tuple((jax.ShapeDtypeStruct(r.shape, r.d...  2.05 us

profile of v3, /device:TPU:0, one launch (start us, length us, event | category | flops | bytes accessed | tf_op | source)
XLA Modules:
  0.0 77.4 jit_solution(2884775874936777878)
XLA Ops:
  0.6 74.7 %shard_map.76 = (bf16[96,2048]{1,0:T(8,128)(2,1)}, bf16[192,1024]{1,0:T(8,128)(2,1)}, bf16[192,1024]{1,0:T(8,128)(2,1)}) custom-call(s32[1,192]{1,0:T(1,128)} %bitcast.1, bf16[192,1024]{1,0:T(8,128)(2,1)} %q_hbm.1, bf16[192,1024]{1,0:T(8,128)(2,1)} %k_hbm.1, bf16[192,1024]{1,0:T(8,128)(2,1)} %v_hbm.1, bf16[192,1024]{1,0:T(8,128)(2,1)} %g_hbm.1), custom_call_target="tpu_custom_call" | custom-call | tf_op jit(solution)/shard_map/pallas_call | solution.py:454
  75.3 2.1 %shard_map.77 = (bf16[96,2048]{1,0:T(8,128)(2,1)}, bf16[192,1024]{1,0:T(8,128)(2,1)}, bf16[192,1024]{1,0:T(8,128)(2,1)}) custom-call(bf16[96,2048]{1,0:T(8,128)(2,1)} %get-tuple-element.6.a_in, bf16[192,1024]{1,0:T(8,128)(2,1)} %get-tuple-element.7.b_in, bf16[192,1024]{1,0:T(8,128)(2,1)} %get-tuple-element.8.c_in), custom_call_target="tpu_custom_call" | custom-call | tf_op jit(solution)/shard_map/pallas_call | solution.py:468

commit v4 on v3

--- a/solution.py
+++ b/solution.py
@@ -12,12 +12,13 @@
 MESH = pl.DeviceIdType.MESH
 NT = (((1,), (1,)), ((), ()))
 LOW = -1e30
+LAG = 6
 PAIR = 2
 STEP = 4
 SEND_OUTER, SEND_INNER = "kCRh", "kCRh"
-STATS_OUTER, STATS_INNER = "CRh", "CRh"
-GRADS_OUTER, GRADS_INNER = "HCR", "RCH"
-BACK_OUTER, BACK_INNER = "rC", "Cr"
+STATS_OUTER, STATS_INNER = ".CRh", ".CRh"
+GRADS_OUTER, GRADS_INNER = "CRH", "CRH"
+BACK_OUTER, BACK_INNER = "RC", "RC"
 
 
 def walk(order, sizes):
@@ -56,52 +57,11 @@
     outer = (2 * mates < ratio) == (2 * line < lines)
     scaling = HEAD_DIM ** (-0.5)
     sharp = scaling / math.log(2.0)
+    slot = (mates * groups + group) * heads + mine
     block = pair * rows
     steps = heads // step
     part_rows = rows // groups
 
-    def by_row(act_outer, act_inner):
-        pl.when(outer)(act_outer)
-        pl.when(jnp.logical_not(outer))(act_inner)
-
-    def columns(index):
-        return pl.ds(pl.multiple_of(index * HEAD_DIM, HEAD_DIM), HEAD_DIM)
-
-    others = [(r, c, e) for r in range(lines) for c in range(across) for e in range(pair)]
-
-    def place_of(r, c):
-        return lax.rem(line + r, lines) * across + lax.rem(column + c, across)
-
-    def ahead(j):
-        r, c, e = others[j]
-        return place_of(r, c) * pair + lax.rem(core + e, pair)
-
-    def behind(j):
-        r, c, e = others[j]
-        return place_of(lines - r, across - c) * pair + lax.rem(core + pair - e, pair)
-
-    def local_copies(arrays, first, stage, sems, j):
-        return [
-            pltpu.make_async_copy(
-                array.at[:, columns(ahead(j))], first.at[a] if j == 0 else stage.at[j, a],
-                sems.at[a, j],
-            )
-            for a, array in enumerate(arrays)
-        ]
-
-    kv_locals = [
-        local_copies((k_hbm, v_hbm), kv_buf.at[mine], kv_stage, kv_local, j)
-        for j in range(heads)
-    ]
-    qg_locals = [
-        local_copies((q_hbm, g_hbm), qg_buf.at[me], qg_stage, qg_local, j) for j in range(heads)
-    ]
-    for copies in kv_locals + qg_locals:
-        for copy in copies:
-            copy.start()
-
-    pos_mine[...] = jnp.zeros_like(pos_mine)
-    pos_mine[:, :rows] = pos_ref[...]
     barrier = pltpu.get_barrier_semaphore()
     for d in range(members):
         for e in range(groups):
@@ -113,6 +73,49 @@
                     },
                     device_id_type=MESH,
                 )
+
+    def by_row(act_outer, act_inner):
+        pl.when(outer)(act_outer)
+        pl.when(jnp.logical_not(outer))(act_inner)
+
+    def columns(index):
+        return pl.ds(pl.multiple_of(index * HEAD_DIM, HEAD_DIM), HEAD_DIM)
+
+    others = [(r, c, e) for r in range(lines) for c in range(across) for e in range(pair)]
+
+    def place_of(r, c):
+        return lax.rem(line + r, lines) * across + lax.rem(column + c, across)
+
+    def ahead(j):
+        r, c, e = others[j]
+        return place_of(r, c) * pair + lax.rem(core + e, pair)
+
+    def behind(j):
+        r, c, e = others[j]
+        return place_of(lines - r, across - c) * pair + lax.rem(core + pair - e, pair)
+
+    def local_copies(arrays, first, stage, sems, j):
+        return [
+            pltpu.make_async_copy(
+                array.at[:, columns(ahead(j))], first.at[a] if j == 0 else stage.at[j, a],
+                sems,
+            )
+            for a, array in enumerate(arrays)
+        ]
+
+    kv_locals = [
+        local_copies((k_hbm, v_hbm), kv_buf.at[mine], kv_stage, kv_local, j)
+        for j in range(heads)
+    ]
+    qg_locals = [
+        local_copies((q_hbm, g_hbm), qg_buf.at[me], qg_stage, qg_local, j) for j in range(heads)
+    ]
+    for copies in kv_locals + qg_locals:
+        for copy in copies:
+            copy.start()
+
+    pos_mine[...] = jnp.zeros_like(pos_mine)
+    pos_mine[:, :rows] = pos_ref[...]
     pl.semaphore_wait(barrier, members * groups - 1)
 
     def remote(source, sink, send, recv, seq, head):
@@ -123,26 +126,28 @@
 
     def pos_copy(d, origin):
         return remote(
-            pos_mine, pos_buf.at[origin], pos_send.at[d], pos_recv.at[origin],
+            pos_mine, pos_buf.at[origin], pos_send, pos_recv,
             lax.rem(me + d, members), group,
         )
 
     def kv_copy(j, origin):
         return remote(
-            kv_stage.at[j], kv_buf.at[origin], kv_send.at[j], kv_recv.at[origin],
+            kv_stage.at[j], kv_buf.at[origin], kv_send, kv_recv,
             mates * heads + ahead(j), group,
         )
 
     def qg_copy(j, d):
         source = qg_buf.at[me] if j == 0 else qg_stage.at[j]
         return remote(
-            source, qg_buf.at[me], qg_send.at[j, d], qg_recv.at[me],
+            source, qg_buf.at[me], qg_send, qg_recv.at[me],
             lax.rem(mates + d, ratio) * heads + ahead(j), group,
         )
 
-    for copies in kv_locals + qg_locals:
-        for copy in copies:
-            copy.wait()
+    def settled(ref, sem):
+        remote(ref, ref, sem, sem, me, group).wait_recv()
+
+    settled(kv_stage, kv_local)
+    settled(qg_stage, qg_local)
     for d in range(1, members):
         pos_copy(d, me).start()
 
@@ -163,8 +168,8 @@
     dk_acc[...] = jnp.zeros_like(dk_acc)
     dv_acc[...] = jnp.zeros_like(dv_acc)
     pos_buf[me] = pos_mine[...]
-    for d in range(1, members):
-        pos_copy(d, lax.rem(me + members - d, members)).wait()
+    settled(pos_buf.at[pl.ds(0, members - 1)], pos_recv)
+    settled(pos_buf.at[pl.ds(0, members - 1)], pos_send)
 
     def spread(i, carry):
         row = jnp.broadcast_to(
@@ -174,8 +179,7 @@
         return carry
 
     lax.fori_loop(0, heads, spread, 0)
-    for j in range(1, heads):
-        kv_copy(j, behind(j)).wait()
+    settled(kv_buf.at[pl.ds(0, heads - 1)], kv_recv)
 
     def turn(s, carry):
         held = kv_buf[pl.ds(s * step, step), 0].reshape(step * rows, HEAD_DIM)
@@ -190,11 +194,31 @@
             value = jnp.where(k == i + 1, entry, value)
         return value
 
-    def unit_of(k, order_outer, order_inner):
-        tables = [
-            [(at["h"] * lines + at["r"]) * across + at["c"] for at in walk(order, sizes)]
-            for order in (order_outer, order_inner)
+    def tables_of(orders):
+        tables = []
+        for order in orders:
+            table = [(at["h"], at["r"], at["c"]) for at in walk(order.strip("."), sizes)]
+            if order.startswith("."):
+                table.insert(0, table.pop(table.index((0, 0, 0))))
+            tables.append(table)
+        return tables
+
+    stats_tables = tables_of((STATS_OUTER, STATS_INNER))
+    grads_tables = tables_of((GRADS_OUTER, GRADS_INNER))
+    lag = max(
+        [LAG]
+        + [
+            there.index(((h - d) % ratio, r, c)) - k
+            for table in grads_tables
+            for k, (h, r, c) in enumerate(table)
+            for there in stats_tables
+            for d in range(ratio)
         ]
+    )
+    lag = min(lag, units)
+
+    def unit_of(k, tables):
+        tables = [[(h * lines + r) * across + c for h, r, c in table] for table in tables]
         n = jnp.where(outer, pick(tables[0], k), pick(tables[1], k))
         there = place_of(lax.rem(n // across, lines), lax.rem(n, across))
         return n, lax.rem(mates + n // wide, ratio) * wide + there
@@ -208,19 +232,19 @@
     def stat_copy(unit, d, origin):
         return remote(
             stat_buf.at[mates, unit], stat_buf.at[origin, unit],
-            stat_send.at[d, unit], stat_recv.at[origin, unit],
+            stat_send, stat_recv.at[origin, unit],
             lax.rem(mates + d, ratio) * heads + mine, group,
         )
 
     def stats(k, carried):
-        n, unit = unit_of(k, STATS_OUTER, STATS_INNER)
+        n, unit = unit_of(k, stats_tables)
         for c in range(pair):
             origin = unit * pair + c
 
             @pl.when(origin != me)
             def _():
                 remote(
-                    qg_buf.at[origin], qg_buf.at[origin], qg_send.at[0, 0], qg_recv.at[origin],
+                    qg_buf.at[origin], qg_buf.at[origin], qg_send, qg_recv.at[origin],
                     me, group,
                 ).wait_recv()
 
@@ -262,12 +286,12 @@
             stat_copy(unit, d, mates).start()
         return carried
 
-    lax.fori_loop(0, units, stats, 0)
+    lax.fori_loop(0, lag, stats, 0)
 
     def grads(k, carried):
-        n, unit = unit_of(k, GRADS_OUTER, GRADS_INNER)
+        n, unit = unit_of(k, grads_tables)
         for d in range(1, ratio):
-            stat_copy(unit, d, lax.rem(mates + ratio - d, ratio)).wait()
+            stat_copy(unit, d, lax.rem(mates + ratio - d, ratio)).wait_recv()
         whole = [stat_buf[d, unit] for d in range(ratio)]
         top = functools.reduce(jnp.maximum, [w[0:1] for w in whole])
         shares = [jnp.exp2((w[0:1] - top) * sharp) for w in whole]
@@ -299,8 +323,8 @@
                 owner = unit * pair + c
                 other = lax.rem(group + e, groups)
                 copy = remote(
-                    dq_stage.at[unit, c, other], dq_back.at[mates, group * heads + mine],
-                    dq_send.at[unit, c, e], dq_recv.at[mates, group * heads + mine],
+                    dq_stage.at[unit, c, other], dq_back.at[slot],
+                    dq_send, dq_recv,
                     owner, other,
                 )
                 if e:
@@ -309,15 +333,22 @@
                     pl.when(owner != me)(copy.start)
         return carried
 
-    lax.fori_loop(0, units, grads, 0)
-
-    dq_back[mates, group * heads + mine] = dq_stage[me // pair, core, group]
+    def both(k, carried):
+        stats(k, 0)
+        grads(k - lag, 0)
+        return carried
+
+    if lag < units:
+        lax.fori_loop(lag, units, both, 0)
+    lax.fori_loop(units - lag, units, grads, 0)
+
+    dq_back[slot] = dq_stage[me // pair, core, group]
 
     def back_copies(j, origin):
         return [
             remote(
-                kv_final.at[j, a], out.at[:, columns(origin)], back_send.at[a, j],
-                back_recv.at[a, origin], mates * heads + ahead(j), group,
+                kv_final.at[j, a], out.at[:, columns(origin)], back_send,
+                back_recv, mates * heads + ahead(j), group,
             )
             for a, out in enumerate((dk_out, dv_out))
         ]
@@ -347,49 +378,22 @@
     for copy in back_locals:
         copy.start()
 
-    for j in range(heads):
-        for d in range(ratio):
-            if j or d:
-                qg_copy(j, d).wait_send()
-
-    def dq_sent(unit, carried):
-        for c in range(pair):
-            for e in range(groups):
-                owner = unit * pair + c
-                other = lax.rem(group + e, groups)
-                copy = remote(
-                    dq_stage.at[unit, c, other], dq_back.at[mates, group * heads + mine],
-                    dq_send.at[unit, c, e], dq_recv.at[mates, group * heads + mine],
-                    owner, other,
-                )
-                if e:
-                    copy.wait_send()
-                else:
-                    pl.when(owner != me)(copy.wait_send)
-        return carried
-
-    lax.fori_loop(0, units, dq_sent, 0)
-
-    for d in range(ratio):
-        for e in range(groups):
-            for i in range(heads):
-                giver = lax.rem(mates + d, ratio)
-                slot = lax.rem(group + e, groups) * heads + lax.rem(mine + i, heads)
-                if d or e or i:
-                    remote(
-                        dq_back.at[giver, slot], dq_back.at[giver, slot],
-                        dq_send.at[0, 0, 0], dq_recv.at[giver, slot], me, group,
-                    ).wait_recv()
+    settled(qg_buf.at[pl.ds(0, members - 1)], qg_send)
+    settled(kv_buf.at[pl.ds(0, heads - 1)], kv_send)
+    settled(stat_buf.at[pl.ds(0, ratio - 1)], stat_send)
+    settled(dq_back.at[pl.ds(0, members * groups - 1)], dq_recv)
     for h in range(groups * heads):
-        parts = [dq_back[d, h].astype(jnp.float32) for d in range(ratio)]
+        parts = [
+            dq_back[d * groups * heads + h].astype(jnp.float32) for d in range(ratio)
+        ]
         dq_sum[:, h * HEAD_DIM:(h + 1) * HEAD_DIM] = functools.reduce(jnp.add, parts).astype(
             jnp.bfloat16
         )
     dq_local = pltpu.make_async_copy(dq_sum, dq_out, dq_own)
     dq_local.start()
-    for j in range(1, heads):
-        for copy in back_copies(j, behind(j)):
-            copy.wait()
+    settled(dq_back.at[pl.ds(0, members * groups - 1)], dq_send)
+    settled(kv_final.at[pl.ds(0, heads - 1)], back_send)
+    settled(kv_final.at[pl.ds(0, heads - 1)], back_recv)
     for copy in back_locals + [dq_local]:
         copy.wait()
 
@@ -442,12 +446,10 @@
         pltpu.VMEM((ratio, units, 8, block), full),
         pltpu.VMEM((heads, 2) + piece, low),
         pltpu.VMEM((units, pair, groups, rows // groups, HEAD_DIM), low),
-        pltpu.VMEM((ratio, groups * heads, rows // groups, HEAD_DIM), low),
+        pltpu.VMEM((members * groups, rows // groups, HEAD_DIM), low),
         pltpu.VMEM((rows // groups, groups * wide), low),
-        dma((2, heads)), dma((2, heads)), dma((heads, ratio)), dma((members,)),
-        dma((heads,)), dma((heads,)), dma((members,)), dma((members,)),
-        dma((ratio, units)), dma((ratio, units)), dma((2, heads)), dma((2, heads)), dma((2,)),
-        dma((units, pair, groups)), dma((ratio, groups * heads)), dma,
+        dma, dma, dma, dma((members,)), dma, dma, dma, dma,
+        dma, dma((ratio, units)), dma, dma, dma((2,)), dma, dma, dma,
     ]
     vmem = pl.BlockSpec(memory_space=pltpu.VMEM)
     hbm = pl.BlockSpec(memory_space=pl.ANY)

time: 77.6 us -> 74.8 us (0.964)
  Pallas kernels: 76.7 us -> 74 us
    pallas_call x1, Pallas kernels: 74.7 us -> 71.9 us  [local(): pl.pallas_call(functools.partial(kernel, members, heads, groups, rows, wi...]
where the time goes in v4:
time: 74.8 us; the launch traced here: 74.6 us
  Pallas kernels  74 us (99%)
    pallas_call x1, Pallas kernels, local(): pl.pallas_call(functools.partial(kernel, members, heads, groups, rows, wi...  71.9 us
    pallas_call x1, Pallas kernels, local(): pl.pallas_call(settle, out_shape=tuple((jax.ShapeDtypeStruct(r.shape, r.d...  2.05 us

profile of v4, /device:TPU:0, one launch (start us, length us, event | category | flops | bytes accessed | tf_op | source)
XLA Modules:
  0.0 74.6 jit_solution(14662247045490666882)
XLA Ops:
  0.6 71.9 %shard_map.76 = (bf16[96,2048]{1,0:T(8,128)(2,1)}, bf16[192,1024]{1,0:T(8,128)(2,1)}, bf16[192,1024]{1,0:T(8,128)(2,1)}) custom-call(s32[1,192]{1,0:T(1,128)} %bitcast.1, bf16[192,1024]{1,0:T(8,128)(2,1)} %q_hbm.1, bf16[192,1024]{1,0:T(8,128)(2,1)} %k_hbm.1, bf16[192,1024]{1,0:T(8,128)(2,1)} %v_hbm.1, bf16[192,1024]{1,0:T(8,128)(2,1)} %g_hbm.1), custom_call_target="tpu_custom_call" | custom-call | tf_op jit(solution)/shard_map/pallas_call | solution.py:456
  72.6 2.1 %shard_map.77 = (bf16[96,2048]{1,0:T(8,128)(2,1)}, bf16[192,1024]{1,0:T(8,128)(2,1)}, bf16[192,1024]{1,0:T(8,128)(2,1)}) custom-call(bf16[96,2048]{1,0:T(8,128)(2,1)} %get-tuple-element.6.a_in, bf16[192,1024]{1,0:T(8,128)(2,1)} %get-tuple-element.7.b_in, bf16[192,1024]{1,0:T(8,128)(2,1)} %get-tuple-element.8.c_in), custom_call_target="tpu_custom_call" | custom-call | tf_op jit(solution)/shard_map/pallas_call | solution.py:470

commit v5 on v4

--- a/solution.py
+++ b/solution.py
@@ -14,7 +14,7 @@
 LOW = -1e30
 LAG = 6
 PAIR = 2
-STEP = 4
+STEP = 8
 SEND_OUTER, SEND_INNER = "kCRh", "kCRh"
 STATS_OUTER, STATS_INNER = ".CRh", ".CRh"
 GRADS_OUTER, GRADS_INNER = "CRH", "CRH"

time: 74.8 us -> 74.2 us (level)
  Pallas kernels: 74 us -> 73 us
    pallas_call x1, Pallas kernels: 71.9 us -> 71 us  [local(): pl.pallas_call(functools.partial(kernel, members, heads, groups, rows, wi...]
where the time goes in v5:
time: 74.2 us; the launch traced here: 73.7 us
  Pallas kernels  73 us (98%)
    pallas_call x1, Pallas kernels, local(): pl.pallas_call(functools.partial(kernel, members, heads, groups, rows, wi...  71 us
    pallas_call x1, Pallas kernels, local(): pl.pallas_call(settle, out_shape=tuple((jax.ShapeDtypeStruct(r.shape, r.d...  2.05 us

profile of v5, /device:TPU:0, one launch (start us, length us, event | category | flops | bytes accessed | tf_op | source)
XLA Modules:
  0.0 73.7 jit_solution(2535421825271433120)
XLA Ops:
  0.6 71.0 %shard_map.76 = (bf16[96,2048]{1,0:T(8,128)(2,1)}, bf16[192,1024]{1,0:T(8,128)(2,1)}, bf16[192,1024]{1,0:T(8,128)(2,1)}) custom-call(s32[1,192]{1,0:T(1,128)} %bitcast.1, bf16[192,1024]{1,0:T(8,128)(2,1)} %q_hbm.1, bf16[192,1024]{1,0:T(8,128)(2,1)} %k_hbm.1, bf16[192,1024]{1,0:T(8,128)(2,1)} %v_hbm.1, bf16[192,1024]{1,0:T(8,128)(2,1)} %g_hbm.1), custom_call_target="tpu_custom_call" | custom-call | tf_op jit(solution)/shard_map/pallas_call | solution.py:456
  71.6 2.1 %shard_map.77 = (bf16[96,2048]{1,0:T(8,128)(2,1)}, bf16[192,1024]{1,0:T(8,128)(2,1)}, bf16[192,1024]{1,0:T(8,128)(2,1)}) custom-call(bf16[96,2048]{1,0:T(8,128)(2,1)} %get-tuple-element.6.a_in, bf16[192,1024]{1,0:T(8,128)(2,1)} %get-tuple-element.7.b_in, bf16[192,1024]{1,0:T(8,128)(2,1)} %get-tuple-element.8.c_in), custom_call_target="tpu_custom_call" | custom-call | tf_op jit(solution)/shard_map/pallas_call | solution.py:470
